TPU v7x, 256 devices: a 8x8x2 block of a 8x8x16 slice. The times are simulated.
256 devices in a mesh: groups: 2 (over z), patch: 128 (over x, y, core).
Axes of the slice: x: 8, y: 8, z: 2, core: 2. Of those that a mesh axis runs over, the one named last changes fastest.
The devices are a block of a 8x8x16 slice.
Arguments:
- queries: bfloat16 [8192, 1536], P(('groups', 'patch')), parts along dimension 0, may hold values from -8 to 8
- fresh_keys: bfloat16 [8192, 1536], P(('groups', 'patch')), parts along dimension 0, may hold values from -8 to 8
- fresh_values: bfloat16 [8192, 1536], P(('groups', 'patch')), parts along dimension 0, may hold values from -128 to 128
- stale_keys: bfloat16 [8192, 1536], P(('groups', 'patch')), parts along dimension 0, may hold values from -8 to 8
- stale_values: bfloat16 [8192, 1536], P(('groups', 'patch')), parts along dimension 0, may hold values from -128 to 128
- text_keys: bfloat16 [452, 1536], P('groups'), parts along dimension 0, may hold values from -8 to 8
- text_values: bfloat16 [452, 1536], P('groups'), parts along dimension 0, may hold values from -128 to 128
- out_weight: bfloat16 [1536, 3072], P(None, 'patch'), may hold values from -0.15625 to 0.15625
- gate_table: float32 [50, 3072], replicated, may hold values from 0.1 to 1.9
- timestep: int32 [2], P('groups'), parts along dimension 0, may hold values from 0 to 49
Outputs:
- branch: bfloat16 [8192, 3072], P(('groups', 'patch')), parts along dimension 0
There are 2 independent parts, one for each index of `groups`. A program takes and returns all parts, laid end to end along the dimension named above; an argument that names none is the same for every part. Nothing has to cross between parts.
All inputs are finite; a program needn't handle non-finite values.
Results may differ from a plain program's by a relative error of at most 0.0095.
Values may be sent and summed in bfloat16 or wider, within the bound.
A program may use at most 128 MiB of HBM per device.

v0:
```python
import jax
import jax.numpy as jnp
from jax import lax
from jax.sharding import PartitionSpec as P

HEAD_DIM = 64
HEADS = 24


def sent_together(arrays, axis, dim, along):
    ends, at = ([], 0)
    for a in arrays[:-1]:
        at += a.shape[along]
        ends.append(at)
    both = jnp.concatenate(arrays, axis=along)
    return tuple(jnp.split(lax.all_gather(both, axis, axis=dim, tiled=True), ends, axis=along))


def body(
    queries,
    fresh_keys,
    fresh_values,
    stale_keys,
    stale_values,
    text_keys,
    text_values,
    out_weight,
    gate_table,
    timestep,
):
    row_count = queries.shape[0]
    head_count = HEADS
    head_width = HEAD_DIM
    scaling = head_width ** (-0.5)
    query = queries.reshape(row_count, head_count, head_width)

    def scores_for(key_block):
        shaped = key_block.reshape(key_block.shape[0], head_count, head_width)
        return (
            jnp.einsum("thd,shd->ths", query, shaped, preferred_element_type=jnp.float32) * scaling
        )

    def weigh(expo, value_block):
        shaped = value_block.reshape(value_block.shape[0], head_count, head_width)
        return jnp.einsum(
            "ths,shd->thd", expo.astype(jnp.bfloat16), shaped, preferred_element_type=jnp.float32
        )

    near_keys = jnp.concatenate([text_keys, fresh_keys], 0)
    near_values = jnp.concatenate([text_values, fresh_values], 0)
    near_scores = scores_for(near_keys)
    running_max = jnp.max(near_scores, -1)
    near_expo = jnp.exp(near_scores - running_max[..., None])
    running_sum = jnp.sum(near_expo, -1)
    weighted = weigh(near_expo, near_values)
    own_first = lax.axis_index("patch") * row_count
    key_part, value_part = sent_together((stale_keys, stale_values), "patch", 0, 1)
    positions = jnp.arange(key_part.shape[0], dtype=jnp.int32)
    remote_mask = (positions < own_first) | (positions >= own_first + row_count)
    scores = jnp.where(remote_mask[None, None, :], scores_for(key_part), -1e30)
    new_max = jnp.maximum(running_max, jnp.max(scores, -1))
    shrink = jnp.exp(running_max - new_max)
    expo = jnp.exp(scores - new_max[..., None])
    new_sum = running_sum * shrink + jnp.sum(expo, -1)
    new_weighted = weighted * shrink[..., None] + weigh(expo, value_part)
    attended = (
        (new_weighted / new_sum[..., None])
        .reshape(row_count, head_count * head_width)
        .astype(jnp.bfloat16)
    )
    projected = jnp.dot(
        attended,
        lax.all_gather(out_weight, "patch", axis=1, tiled=True),
        preferred_element_type=jnp.float32,
    )
    selector = (jnp.arange(gate_table.shape[0], dtype=jnp.int32) == timestep[0]).astype(jnp.float32)
    gating = jnp.dot(selector, gate_table, precision=lax.Precision.HIGHEST)
    return (projected * gating[None, :]).astype(jnp.bfloat16)


def solution(mesh):
    in_specs = (
        P(("groups", "patch"), None),
        P(("groups", "patch"), None),
        P(("groups", "patch"), None),
        P(("groups", "patch"), None),
        P(("groups", "patch"), None),
        P("groups", None),
        P("groups", None),
        P(None, "patch"),
        P(),
        P("groups"),
    )
    out_specs = P(("groups", "patch"), None)
    return jax.shard_map(body, mesh=mesh, in_specs=in_specs, out_specs=out_specs, check_vma=False)
```

profile of v0, /device:TPU:513, one launch (start us, length us, event | category | flops | bytes accessed | tf_op | source)
XLA Modules:
  0.0 246.7 jit_solution(3291035466819410238)
XLA Ops:
  6.5 0.0 copy-start
  6.6 0.0 all-gather.3.cloned.1.call-start
  6.6 1.7 pad_maximum_fusion.2
  8.3 0.1 all-gather.3.cloned.1.call-update
  8.3 0.1 all-gather.5.cloned.1.call-start
  8.4 0.7 all-gather.5.cloned.1.call-update
  9.1 1.1 reshape.49
  10.2 1.2 pad_maximum_fusion.1
  11.4 0.7 copy.18
  12.2 1.2 pad_maximum_fusion
  13.4 1.4 copy.17
  15.5 0.4 fusion.34
  15.9 0.4 fusion.18
  16.3 0.0 copy-done
  16.3 0.3 fusion.26
  16.6 129.8 %all-gather.3.cloned.1.call-done = bf16[4096,3072]{1,0:T(8,128)(2,1)} async-done(((bf16[32,3072]{1,0:T(8,128)(2,1)}), bf16[4096,3072]{1,0:T(8,128)(2,1)}) %all-gather.3.cloned.1.call-update) | async-done | bytes 25165840 | tf_op jit(solution)/shard_map/all_gather | solution.py:16
  146.4 17.1 %fusion.33 = (bf16[4096,1536]{1,0:T(8,128)(2,1)}, bf16[4096,1536]{1,0:T(8,128)(2,1)}) fusion(bf16[4096,3072]{1,0:T(8,128)(2,1)} %all-gather.3.cloned.1.call-done), kind=kLoop, calls=%fused_computation.43 | loop fusion | bytes 50331648 | tf_op jit(solution)/shard_map/split | solution.py:16
  163.5 16.4 %copy.22 = bf16[4096,1536]{0,1:T(8,128)(2,1)} copy(bf16[4096,1536]{1,0:T(8,128)(2,1)} %get-tuple-element.8) | data formatting | bytes 25165824 | tf_op jit(solution)/shard_map/split | solution.py:16
  179.9 16.8 %copy.20 = bf16[4096,1536]{0,1:T(8,128)(2,1)} copy(bf16[4096,1536]{1,0:T(8,128)(2,1)} %get-tuple-element.7) | data formatting | bytes 25165824 | tf_op jit(solution)/shard_map/split | solution.py:16
  196.7 6.4 %bitcast_reduce_fusion = (f32[32,24]{0,1:T(8,128)S(1)}, f32[24,4096,32]{1,2,0:T(8,128)S(1)}) fusion(pred[4096]{0:T(1024)(128)(4,1)S(1)} %fusion.25, bf16[4096,24,64]{0,2,1:T(8,128)(2,1)} %bitcast.43, bf16[32,24,64]{2,1,0:T(8,128)(2,1)S(1)} %reshape.49), kind=kOutput, calls=%fused_computation.1 | convolution fusion | flops 412089600 | bytes 25271296 | tf_op jit(solution)/shard_map/thd,shd->ths/dot_general | solution.py:40
  203.1 4.6 %copy-done.2 = f32[24,4096,32]{1,2,0:T(8,128)} copy-done((f32[24,4096,32]{1,2,0:T(8,128)}, f32[24,4096,32]{1,2,0:T(8,128)S(1)}, u32[]{:S(2)}) %copy-start.2) | copy-done | bytes 12582936
  207.7 3.0 %fusion.1 = f32[32,24]{0,1:T(8,128)S(1)} fusion(f32[24,4096,32]{1,2,0:T(8,128)S(1)} %get-tuple-element.12, f32[32,24]{0,1:T(8,128)S(1)} %max.13, pred[4096]{0:T(1024)(128)(4,1)S(1)} %fusion.25), kind=kLoop, calls=%fused_computation.4 | loop fusion | flops 12582144 | bytes 12593152 | tf_op jit(solution)/shard_map/reduce_sum | solution.py:64
  210.8 0.0 copy-start.3
  210.8 0.0 copy-start.1
  210.8 11.1 %fusion.14 = f32[32,24,64]{2,0,1:T(8,128)S(1)} fusion(bf16[4096,24,64]{0,2,1:T(8,128)(2,1)} %bitcast.44, f32[24,4096,32]{1,2,0:T(8,128)} %copy-done.2, f32[32,24]{0,1:T(8,128)S(1)} %max.13, pred[4096]{0:T(1024)(128)(4,1)S(1)} %fusion.25), kind=kOutput, calls=%fused_computation.19 | convolution fusion | flops 415236096 | bytes 25369600 | tf_op jit(solution)/shard_map/ths,shd->thd/dot_general | solution.py:45
  221.9 0.0 copy-done.3
  221.9 0.6 fusion.17
  222.5 0.1 copy.23
  222.6 0.2 convert_element_type.19
  222.8 9.8 %all-gather.5.cloned.1.call-done = bf16[1536,3072]{0,1:T(8,128)(2,1)} async-done(((bf16[1536,24]{0,1:T(8,128)(2,1)}), bf16[1536,3072]{0,1:T(8,128)(2,1)}) %all-gather.5.cloned.1.call-update) | async-done | bytes 9437200 | tf_op jit(solution)/shard_map/all_gather | solution.py:73
  232.6 7.2 %fusion.9 = bf16[32,3072]{1,0:T(8,128)(2,1)} fusion(bf16[32,1536]{1,0:T(8,128)(2,1)S(1)} %convert_element_type.19, bf16[1536,3072]{0,1:T(8,128)(2,1)} %all-gather.5.cloned.1.call-done, f32[3072]{0:T(1024)S(1)} %bitcast.47), kind=kOutput, calls=%fused_computation.12 | convolution fusion | flops 302186496 | bytes 9744384 | tf_op jit(solution)/shard_map/dot_general | solution.py:71
  239.8 0.0 copy-done.1
  (4 shorter events, 0.0 us)
Async XLA Ops:
  6.5 9.7 %copy-start = (f32[50,3072]{1,0:T(8,128)S(1)}, f32[50,3072]{1,0:T(8,128)}, u32[]{:S(2)}) copy-start(f32[50,3072]{1,0:T(8,128)} %param.18) | copy-start | bytes 1843204
  6.6 139.9 %all-gather.3.cloned.1.call-start = ((), (), s32[]{:S(2)}) async-start(), calls=%async_computation | async-start | bytes 25362432 | tf_op jit(solution)/shard_map/all_gather | solution.py:16
  8.3 224.3 %all-gather.5.cloned.1.call-start = ((), (), s32[]{:S(2)}) async-start(), calls=%async_computation.1 | async-start | bytes 9510912 | tf_op jit(solution)/shard_map/all_gather | solution.py:73
  203.1 4.6 %copy-start.2 = (f32[24,4096,32]{1,2,0:T(8,128)}, f32[24,4096,32]{1,2,0:T(8,128)S(1)}, u32[]{:S(2)}) copy-start(f32[24,4096,32]{1,2,0:T(8,128)S(1)} %get-tuple-element.12) | copy-start | bytes 37748740
  210.8 11.2 %copy-start.3 = (bf16[258,1536]{0,1:T(8,128)(2,1)S(1)}, bf16[258,1536]{0,1:T(8,128)(2,1)}, u32[]{:S(2)}) copy-start(bf16[258,1536]{0,1:T(8,128)(2,1)} %copy.17) | copy-start | bytes 2377732
  210.8 29.1 %copy-start.1 = (f32[50,3072]{1,0:T(8,128)S(1)}, f32[50,3072]{1,0:T(8,128)}, u32[]{:S(2)}) copy-start(f32[50,3072]{1,0:T(8,128)} %param.18) | copy-start | bytes 1843204
Sparse Core Ops, SparseCore 0:
  9.9 136.4 all-gather.2
  149.0 83.5 all-gather.4
where the time goes:
time: 248 us; the launch traced here: 247 us
  waiting for transfers between devices  140 us (56%)
  local copies, waits for them, and re-layouts  58.3 us (24%)
  matrix products  26.1 us (11%)
  between operations  14.2 us (6%)
  other arithmetic  7.58 us (3%)
    all_gather x1, waiting for transfers between devices, sent_together(): lax.all_gather(both, axis, axis=dim, tiled=True)  130 us
    split x3, local copies, waits for them, and re-layouts, sent_together(): jnp.split(lax.all_gather(both, axis, axis=dim, tiled=True), ends, axis=al...  50.3 us
    dot_general x2, matrix products, weigh(): jnp.einsum('ths,shd->thd', expo.astype(jnp.bfloat16), shaped, preferred_e...  11.7 us
    all_gather x1, waiting for transfers between devices, body(): lax.all_gather(out_weight, 'patch', axis=1, tiled=True)  9.83 us
    dot_general x1, matrix products, body(): jnp.dot(attended, lax.all_gather(out_weight, 'patch', axis=1, tiled=True)...  7.19 us
    dot_general x2, matrix products, scores_for(): jnp.einsum('thd,shd->ths', query, shaped, preferred_element_type=jnp.floa...  6.84 us
  transfers between devices with their start and end apart: 2, of which 2 were waited for; matrix products, arithmetic and copies ran while one was open for 32% of the time, Pallas kernels for 0%

commit v1 on v0

--- a/solution.py
+++ b/solution.py
@@ -68,10 +68,11 @@
         .reshape(row_count, head_count * head_width)
         .astype(jnp.bfloat16)
     )
+    supply_all_shards_in = lambda here_x: jnp.concatenate(
+        lax.all_to_all(jnp.stack(lax.axis_size("patch") * [here_x], 0), "patch", 0, 0), 1
+    )
     projected = jnp.dot(
-        attended,
-        lax.all_gather(out_weight, "patch", axis=1, tiled=True),
-        preferred_element_type=jnp.float32,
+        attended, supply_all_shards_in(out_weight), preferred_element_type=jnp.float32
     )
     selector = (jnp.arange(gate_table.shape[0], dtype=jnp.int32) == timestep[0]).astype(jnp.float32)
     gating = jnp.dot(selector, gate_table, precision=lax.Precision.HIGHEST)

time: 248 us -> 475 us (1.92)
  waiting for transfers between devices: 140 us -> 338 us
  starting transfers between devices: 0.07 us -> 28.5 us
    all_gather x1, waiting for transfers between devices: 130 us -> 338 us  [sent_together(): lax.all_gather(both, axis, axis=dim, tiled=True)]
    all_to_all x0 -> x1, starting transfers between devices: none -> 28.5 us  [body(): lax.all_to_all(jnp.stack(lax.axis_size('patch') * [here_x], 0), 'patch',...]
    all_gather x1 -> x0, waiting for transfers between devices: 9.83 us -> none  [body(): lax.all_gather(out_weight, 'patch', axis=1, tiled=True)]
    another operation x0 -> x1, local copies, waits for them, and re-layouts: none -> 5.11 us  [body(): jnp.stack(lax.axis_size('patch') * [here_x], 0)]
  transfers between devices with their start and end apart: 2 -> 2, of which waited for: 2 -> 1; matrix products, arithmetic and copies ran while one was open for 32% -> 17% of each run, Pallas kernels for 0% -> 0%
where the time goes in v1:
time: 475 us; the launch traced here: 474 us
  waiting for transfers between devices  338 us (71%)
  local copies, waits for them, and re-layouts  62.7 us (13%)
  starting transfers between devices  28.5 us (6%)
  matrix products  24.8 us (5%)
  between operations  14.3 us (3%)
  other arithmetic  6.38 us (1%)
    all_gather x1, waiting for transfers between devices, sent_together(): lax.all_gather(both, axis, axis=dim, tiled=True)  338 us
    split x3, local copies, waits for them, and re-layouts, sent_together(): jnp.split(lax.all_gather(both, axis, axis=dim, tiled=True), ends, axis=al...  50.5 us
    all_to_all x1, starting transfers between devices, body(): lax.all_to_all(jnp.stack(lax.axis_size('patch') * [here_x], 0), 'patch',...  28.5 us
    dot_general x2, matrix products, weigh(): jnp.einsum('ths,shd->thd', expo.astype(jnp.bfloat16), shaped, preferred_e...  10.8 us
  transfers between devices with their start and end apart: 2, of which 1 were waited for; matrix products, arithmetic and copies ran while one was open for 17% of the time, Pallas kernels for 0%

profile of v1, /device:TPU:513, one launch (start us, length us, event | category | flops | bytes accessed | tf_op | source)
XLA Modules:
  0.0 474.3 jit_solution(1568323492249783316)
XLA Ops:
  6.5 0.0 copy-start
  6.6 1.7 pad_maximum_fusion.2
  8.3 0.1 all-gather.2.cloned.1.call-update
  8.3 0.0 copy-start.7
  8.3 0.0 copy-start.4
  8.3 0.0 copy-start.5
  8.3 5.1 %stack.2 = bf16[128,1536,24]{1,2,0:T(8,128)(2,1)} broadcast(bf16[1536,24]{0,1:T(8,128)(2,1)} %param.17), dimensions={1,2} | broadcast | bytes 9510912 | tf_op jit(solution)/shard_map/stack | solution.py:72
  13.5 28.5 %all-to-all-start = ((bf16[128,1536,24]{1,2,0:T(8,128)(2,1)}), bf16[128,1536,24]{1,2,0:T(8,128)(2,1)}, u32[]{:S(2)}, u32[]{:S(2)}) async-start(bf16[128,1536,24]{1,2,0:T(8,128)(2,1)} %stack.2), calls=%async_computation | async-start | bytes 18874368 | tf_op jit(solution)/shard_map/all_to_all | solution.py:72
  42.0 0.2 reshape.57
  42.2 0.1 pad_maximum_fusion.1
  42.2 0.7 copy.19
  43.0 0.0 copy-done.6
  43.0 1.2 pad_maximum_fusion
  44.2 1.4 copy.18
  46.2 0.4 fusion.34
  46.6 0.4 fusion.18
  47.0 0.0 copy-done
  47.0 0.3 fusion.26
  47.4 337.7 %all-gather.2.cloned.1.call-done = bf16[4096,3072]{1,0:T(8,128)(2,1)} async-done(((bf16[32,3072]{1,0:T(8,128)(2,1)}), bf16[4096,3072]{1,0:T(8,128)(2,1)}) %all-gather.2.cloned.1.call-update) | async-done | bytes 25165840 | tf_op jit(solution)/shard_map/all_gather | solution.py:16
  385.1 17.1 %fusion.33 = (bf16[4096,1536]{1,0:T(8,128)(2,1)}, bf16[4096,1536]{1,0:T(8,128)(2,1)}) fusion(bf16[4096,3072]{1,0:T(8,128)(2,1)} %all-gather.2.cloned.1.call-done), kind=kLoop, calls=%fused_computation.43 | loop fusion | bytes 50331648 | tf_op jit(solution)/shard_map/split | solution.py:16
  402.2 16.6 %copy.23 = bf16[4096,1536]{0,1:T(8,128)(2,1)} copy(bf16[4096,1536]{1,0:T(8,128)(2,1)} %get-tuple-element.8) | data formatting | bytes 25165824 | tf_op jit(solution)/shard_map/split | solution.py:16
  418.8 16.8 %copy.21 = bf16[4096,1536]{0,1:T(8,128)(2,1)} copy(bf16[4096,1536]{1,0:T(8,128)(2,1)} %get-tuple-element.7) | data formatting | bytes 25165824 | tf_op jit(solution)/shard_map/split | solution.py:16
  435.6 6.0 %bitcast_reduce_fusion = (f32[32,24]{0,1:T(8,128)S(1)}, f32[24,4096,32]{1,2,0:T(8,128)S(1)}) fusion(pred[4096]{0:T(1024)(128)(4,1)S(1)} %fusion.25, bf16[4096,24,64]{0,2,1:T(8,128)(2,1)} %bitcast.46, bf16[32,24,64]{2,1,0:T(8,128)(2,1)S(1)} %reshape.57), kind=kOutput, calls=%fused_computation.1 | convolution fusion | flops 412089600 | bytes 25271296 | tf_op jit(solution)/shard_map/thd,shd->ths/dot_general | solution.py:40
  441.6 4.5 copy-done.2
  446.1 3.0 fusion.1
  449.1 0.0 copy-start.1
  449.1 10.1 %fusion.14 = f32[32,24,64]{2,0,1:T(8,128)S(1)} fusion(bf16[4096,24,64]{0,2,1:T(8,128)(2,1)} %bitcast.47, f32[24,4096,32]{1,2,0:T(8,128)} %copy-done.2, f32[32,24]{0,1:T(8,128)S(1)} %max.13, pred[4096]{0:T(1024)(128)(4,1)S(1)} %fusion.25), kind=kOutput, calls=%fused_computation.19 | convolution fusion | flops 415236096 | bytes 25369600 | tf_op jit(solution)/shard_map/ths,shd->thd/dot_general | solution.py:45
  459.3 0.6 fusion.17
  459.9 0.1 copy.24
  460.0 0.2 convert_element_type.19
  460.2 0.0 all-to-all-done
  460.2 7.2 %fusion.9 = bf16[32,3072]{1,0:T(8,128)(2,1)} fusion(bf16[32,1536]{1,0:T(8,128)(2,1)S(1)} %convert_element_type.19, bf16[1536,3072]{0,1:T(8,128)(2,1)} %bitcast.9, f32[3072]{0:T(1024)S(1)} %bitcast.50), kind=kOutput, calls=%fused_computation.12 | convolution fusion | flops 302186496 | bytes 9744384 | tf_op jit(solution)/shard_map/dot_general | solution.py:74
  (12 shorter events, 0.0 us)
Async XLA Ops:
  6.5 40.5 %copy-start = (f32[50,3072]{1,0:T(8,128)S(1)}, f32[50,3072]{1,0:T(8,128)}, u32[]{:S(2)}) copy-start(f32[50,3072]{1,0:T(8,128)} %param.18) | copy-start | bytes 1843204
  6.6 378.5 %all-gather.2.cloned.1.call-start = ((), (), s32[]{:S(2)}) async-start(), calls=%async_computation.1 | async-start | bytes 25362432 | tf_op jit(solution)/shard_map/all_gather | solution.py:16
  8.3 33.7 %copy-start.7 = (bf16[32,1536]{1,0:T(8,128)(2,1)S(1)}, bf16[32,1536]{1,0:T(8,128)(2,1)}, u32[]{:S(2)}) copy-start(bf16[32,1536]{1,0:T(8,128)(2,1)} %param.10) | copy-start | bytes 294916
  8.3 33.8 %copy-start.4 = (bf16[226,1536]{1,0:T(8,128)(2,1)S(1)}, bf16[226,1536]{1,0:T(8,128)(2,1)}, u32[]{:S(2)}) copy-start(bf16[226,1536]{1,0:T(8,128)(2,1)} %param.15) | copy-start | bytes 2082820
  8.3 33.8 %copy-start.5 = (bf16[32,1536]{1,0:T(8,128)(2,1)S(1)}, bf16[32,1536]{1,0:T(8,128)(2,1)}, u32[]{:S(2)}) copy-start(bf16[32,1536]{1,0:T(8,128)(2,1)} %param.11) | copy-start | bytes 294916
  13.5 29.5 %copy-start.6 = (bf16[32,1536]{1,0:T(8,128)(2,1)S(1)}, bf16[32,1536]{1,0:T(8,128)(2,1)}, u32[]{:S(2)}) copy-start(bf16[32,1536]{1,0:T(8,128)(2,1)} %param.12) | copy-start | bytes 294916
  13.5 446.7 %all-to-all-start = ((bf16[128,1536,24]{1,2,0:T(8,128)(2,1)}), bf16[128,1536,24]{1,2,0:T(8,128)(2,1)}, u32[]{:S(2)}, u32[]{:S(2)}) async-start(bf16[128,1536,24]{1,2,0:T(8,128)(2,1)} %stack.2), calls=%async_computation | async-start | bytes 18874368 | tf_op jit(solution)/shard_map/all_to_all | solution.py:72
  441.6 4.5 copy-start.2
  449.1 10.2 %copy-start.3 = (bf16[258,1536]{0,1:T(8,128)(2,1)S(1)}, bf16[258,1536]{0,1:T(8,128)(2,1)}, u32[]{:S(2)}) copy-start(bf16[258,1536]{0,1:T(8,128)(2,1)} %copy.18) | copy-start | bytes 2377732
  449.1 18.3 %copy-start.1 = (f32[50,3072]{1,0:T(8,128)S(1)}, f32[50,3072]{1,0:T(8,128)}, u32[]{:S(2)}) copy-start(f32[50,3072]{1,0:T(8,128)} %param.18) | copy-start | bytes 1843204
Sparse Core Ops, SparseCore 0:
  9.9 375.0 all-gather.1
